TPU v7x, 32 devices: a whole 2x2x4 slice. The times are simulated.
32 devices in a mesh: gx: 4 (over y, x), gz: 8 (over z, core).
Axes of the slice: x: 2, y: 2, z: 4, core: 2. Of those that a mesh axis runs over, the one named last changes fastest.
Arguments:
- divergence: float32 [256, 128, 512], P('gx', 'gz'), may hold values from -18 to 18
- level_set: float32 [256, 128, 512], P('gx', 'gz'), may hold values from -2 to 2, as said below
- tile_ids: int32 [4, 8192], P('gx', 'gz'), may hold values from -1 to 1023, as said below
Outputs:
- pressure: float32 [256, 128, 512], P('gx', 'gz')
- residual: float32 [256, 128, 512], P('gx', 'gz')
Inputs may be any that keep to these rules, and one draw needn't show every extreme that they name: `level_set`: every entry lies at least 0.05 away from zero. `tile_ids`: each device's part lists distinct tile numbers of its own block, below 1024, in increasing order, followed by -1 entries; some device lists all 1024 and some device lists none.
All inputs are finite; a program needn't handle non-finite values.
Results may differ from a plain program's by a relative error of at most 0.0003.
Values sent between devices are 32-bit elements; how exact they have to be, the bound alone decides.
No kernel may reach another device: no remote copies, remote signals or barrier semaphores. Data moves between devices by JAX's collectives and lax.ppermute only.
A program may use at most 128 MiB of HBM per device.

v0:
```python
import jax
import jax.numpy as jnp
from jax import lax
from jax.sharding import PartitionSpec as P

ITERS = 2
TILE = 8
damping = 2.0 / 3.0
ratio_cap = 20.0


def with_halo(block, sides, width):
    for axis, dim in sides:
        count = lax.axis_size(axis)
        forward = [(i, i + 1) for i in range(count - 1)]
        backward = [(target, source) for source, target in forward]
        low = lax.ppermute(
            lax.slice_in_dim(block, block.shape[dim] - width, None, axis=dim), axis, forward
        )
        high = lax.ppermute(lax.slice_in_dim(block, 0, width, axis=dim), axis, backward)
        block = jnp.concatenate([low, block, high], axis=dim)
    return block


def beside(values):
    center = values[1:-1, 1:-1]
    upward = jnp.concatenate([center[:, :, 1:], jnp.zeros_like(center[:, :, :1])], 2)
    downward = jnp.concatenate([jnp.zeros_like(center[:, :, :1]), center[:, :, :-1]], 2)
    return [
        values[2:, 1:-1],
        values[:-2, 1:-1],
        values[1:-1, 2:],
        values[1:-1, :-2],
        upward,
        downward,
    ]


def beside_all(values):
    pieces = beside(values)
    result = pieces[0] + pieces[1]
    for addend in pieces[2:]:
        result = result + addend
    return result


def coefficients(dist_ext, fluid_ext):
    dist_mid = dist_ext[1:-1, 1:-1]
    fluid_mid = fluid_ext[1:-1, 1:-1]
    safe_dist = jnp.where(dist_mid > 0, dist_mid, 1.0)
    term_list = [
        jnp.where(fluid_side > 0, 1.0, jnp.minimum((dist_mid + dist_side) / safe_dist, ratio_cap))
        for dist_side, fluid_side in zip(beside(dist_ext), beside(fluid_ext))
    ]
    result = term_list[0] + term_list[1]
    for addend in term_list[2:]:
        result = result + addend
    return (jnp.where(fluid_mid > 0, result, 1.0), fluid_mid)


def on_device(divergence, level_set, tile_ids):
    size_x, size_z, size_y = divergence.shape
    tiles_x, tiles_z, tiles_y = (size_x // TILE, size_z // TILE, size_y // TILE)
    listed = tile_ids.reshape(-1)
    numbers = lax.broadcasted_iota(jnp.int32, (1, tiles_x * tiles_z * tiles_y), 1)
    listed_hit = (
        jnp.any(listed[:, None] == numbers, axis=0)
        .astype(jnp.float32)
        .reshape(tiles_x, tiles_z, tiles_y)
    )
    active = jnp.broadcast_to(
        listed_hit[:, None, :, None, :, None], (tiles_x, TILE, tiles_z, TILE, tiles_y, TILE)
    ).reshape(size_x, size_z, size_y)
    fluid_cells = jnp.where(level_set < 0, active, 0.0)
    distance = jnp.abs(level_set)
    stacked = jnp.stack((distance, fluid_cells))
    near_cells = with_halo(stacked, (("gx", 1), ("gz", 2)), 1)
    diag_mid, fluid_mid = coefficients(near_cells[0], near_cells[1])
    scale_mid = damping / diag_mid

    def operate(values):
        padded = with_halo(values, (("gx", 0), ("gz", 1)), 1)
        return fluid_mid * (diag_mid * values - beside_all(padded))

    def precondition(residual):
        first_pass = scale_mid * residual
        second_pass = first_pass + scale_mid * (residual - operate(first_pass))
        return (second_pass, operate(second_pass))

    pressure = jnp.zeros_like(divergence)
    residual = fluid_mid * divergence
    smoothed, precond_image = precondition(residual)
    direction = smoothed
    operated = precond_image

    def both_sums(current, preconditioned, image_of):
        return lax.psum(
            (jnp.sum(current * preconditioned), jnp.sum(image_of * preconditioned)), ("gx", "gz")
        )

    gamma_now, delta_now = both_sums(residual, smoothed, precond_image)
    alpha_now = gamma_now / delta_now
    for iteration in range(ITERS):
        pressure = pressure + alpha_now * direction
        residual = residual - alpha_now * operated
        if iteration + 1 < ITERS:
            smoothed, precond_image = precondition(residual)
            gamma_next, delta_now = both_sums(residual, smoothed, precond_image)
            beta_now = gamma_next / gamma_now
            alpha_now = gamma_next / (delta_now - beta_now * gamma_next / alpha_now)
            direction = smoothed + beta_now * direction
            operated = precond_image + beta_now * operated
            gamma_now = gamma_next
    return (pressure, residual)


def solution(mesh):
    placed = (P("gx", "gz", None), P("gx", "gz", None), P("gx", "gz"))
    return jax.shard_map(
        on_device,
        mesh=mesh,
        in_specs=placed,
        out_specs=(P("gx", "gz", None), P("gx", "gz", None)),
        check_vma=False,
    )
```

profile of v0, /device:TPU:0, one launch (start us, length us, event | category | flops | bytes accessed | tf_op | source)
XLA Modules:
  0.0 272.1 jit_solution(12472779404348531436)
XLA Ops:
  2.0 11.3 %broadcast_in_dim.18 = f32[8,8,2,8,64,8]{5,4,3,2,1,0:T(8,128)} broadcast(f32[8,2,64]{2,1,0:T(2,128)S(1)} %reshape.16), dimensions={0,2,4} | broadcast | bytes 2101248 | tf_op jit(solution)/shard_map/broadcast_in_dim | solution.py:71
  13.4 25.1 %reshape.15 = f32[64,16,512]{2,1,0:T(8,128)} reshape(f32[8,8,2,8,64,8]{5,4,3,2,1,0:T(8,128)} %broadcast_in_dim.18) | data formatting | bytes 4194304 | tf_op jit(solution)/shard_map/reshape | solution.py:73
  38.4 3.0 %abs_bitcast_fusion = (f32[1,64,16,512]{3,2,1,0:T(8,128)S(1)}, f32[1,64,16,512]{3,2,1,0:T(8,128)S(1)}) fusion(f32[64,16,512]{2,1,0:T(8,128)} %param.4, f32[64,16,512]{2,1,0:T(8,128)} %reshape.15), kind=kLoop, calls=%fused_computation.114 | loop fusion | flops 1572864 | bytes 8388608 | tf_op jit(solution)/shard_map/stack | solution.py:76
  41.4 4.9 %collective-permute-start = (f32[2,1,16,512]{3,2,1,0:T(8,128)S(1)}, f32[2,1,16,512]{3,2,1,0:T(8,128)S(1)}, u32[]{:S(2)}, u32[]{:S(2)}) collective-permute-start(f32[2,1,16,512]{3,2,1,0:T(8,128)S(1)} %get-tuple-element.21), channel_id=1, source_target_pairs={{0,8},{8,16},{16,24},{1,9},{9,17},{17,25},{2,10},{10,18},{18,26},{... | collective-permute-start | bytes 196616 | tf_op jit(solution)/shard_map/ppermute | solution.py:17
  48.2 4.3 %collective-permute-done.1 = f32[2,1,16,512]{3,2,1,0:T(8,128)S(1)} collective-permute-done((f32[2,1,16,512]{3,2,1,0:T(8,128)S(1)}, f32[2,1,16,512]{3,2,1,0:T(8,128)S(1)}, u32[]{:S(2)}, u32[]{:S(2)}) %collective-permute-start.1) | collective-permute-done | bytes 65568 | tf_op jit(solution)/shard_map/ppermute | solution.py:20
  53.0 1.3 collective-permute-start.2
  55.6 3.9 %collective-permute-done.3 = f32[2,66,1,512]{3,2,1,0:T(1,128)S(1)} collective-permute-done((f32[2,66,1,512]{3,2,1,0:T(1,128)S(1)}, f32[2,66,1,512]{3,2,1,0:T(1,128)S(1)}, u32[]{:S(2)}, u32[]{:S(2)}) %collective-permute-start.3) | collective-permute-done | bytes 270368 | tf_op jit(solution)/shard_map/ppermute | solution.py:20
  59.6 2.5 pad_maximum_fusion
  62.8 5.4 %fusion.64 = (f32[64,16,511]{2,1,0:T(8,128)}, f32[64,16,511]{2,1,0:T(8,128)}, f32[64,16,511]{2,1,0:T(8,128)}, f32[64,16,511]{2,1,0:T(8,128)}) fusion(f32[66,18,512]{2,1,0:T(8,128)S(1)} %get-tuple-element.17, f32[66,18,512]{2,1,0:T(8,128)S(1)} %get-tuple-element.18), kind=kLoop, calls=%fused_computation.137 | loop fusion | bytes 16744448 | tf_op jit(solution)/shard_map/slice | solution.py:27
  68.2 8.7 %fusion.60 = (f32[64,16,512]{2,1,0:T(8,128)}, f32[64,16,512]{2,1,0:T(8,128)S(1)}, f32[64,16,512]{2,1,0:T(8,128)}) fusion(f32[64,16,511]{2,1,0:T(8,128)} %get-tuple-element.53, f32[64,16,511]{2,1,0:T(8,128)} %get-tuple-element.24, f32[64,16,511]{2,1,0:T(8,128)} %get-tuple-element.54, f32[64,16,511]{2,1,0:T(8,128)} %get-tuple-element.23, ...), kind=kLoop, calls=%fused_computation.118 | loop fusion | flops 22020096 | bytes 37732352 | tf_op jit(solution)/shard_map/mul | solution.py:86
  77.9 4.4 %collective-permute-start.5 = (f32[1,16,512]{2,1,0:T(8,128)S(1)}, f32[1,16,512]{2,1,0:T(8,128)S(1)}, u32[]{:S(2)}, u32[]{:S(2)}) collective-permute-start(f32[1,16,512]{2,1,0:T(8,128)S(1)} %get-tuple-element.49), channel_id=1, source_target_pairs={{0,8},{8,16},{16,24},{1,9},{9,17},{17,25},{2,10},{10,18},{18,26},{... | collective-permute-start | bytes 98312 | tf_op jit(solution)/shard_map/ppermute | solution.py:17
  83.9 4.2 %collective-permute-done.4 = f32[1,16,512]{2,1,0:T(8,128)S(1)} collective-permute-done((f32[1,16,512]{2,1,0:T(8,128)S(1)}, f32[1,16,512]{2,1,0:T(8,128)S(1)}, u32[]{:S(2)}, u32[]{:S(2)}) %collective-permute-start.4) | collective-permute-done | bytes 32800 | tf_op jit(solution)/shard_map/ppermute | solution.py:20
  88.2 1.8 pad_maximum_fusion.48
  91.3 6.3 %collective-permute-start.7 = (f32[66,1,512]{2,1,0:T(1,128)S(1)}, f32[66,1,512]{2,1,0:T(1,128)S(1)}, u32[]{:S(2)}, u32[]{:S(2)}) collective-permute-start(f32[66,1,512]{2,1,0:T(1,128)S(1)} %get-tuple-element.34), channel_id=1, source_target_pairs={{0,1},{1,2},{2,3},{3,4},{4,5},{5,6},{6,7},{8,9},{9,10},{10,11},{11... | collective-permute-start | bytes 405512 | tf_op jit(solution)/shard_map/ppermute | solution.py:17
  98.4 4.2 %fusion.32 = f32[64,16,512]{2,1,0:T(8,128)S(1)} fusion(f32[64,16,512]{2,1,0:T(8,128)S(1)} %copy-done.4, f32[64,16,512]{2,1,0:T(8,128)S(1)} %copy-done.7, f32[66,1,512]{2,1,0:T(1,128)S(1)} %collective-permute-done.7, f32[1,16,512]{2,1,0:T(8,128)S(1)} %collective-permute-done.4, f32[1,16,512]{2,1,0:T(8,128)S(1)} %collective-permute-done.5, ...), kind=kLoop, calls=%fused_computation.62 | loop fusion | flops 10485760 | bytes 15007744 | tf_op jit(solution)/shard_map/add | solution.py:87
  102.7 3.4 %collective-permute-start.9 = (f32[1,16,512]{2,1,0:T(8,128)S(1)}, f32[1,16,512]{2,1,0:T(8,128)S(1)}, u32[]{:S(2)}, u32[]{:S(2)}) collective-permute-start(f32[1,16,512]{2,1,0:T(8,128)S(1)} %get-tuple-element.43), channel_id=1, source_target_pairs={{0,8},{8,16},{16,24},{1,9},{9,17},{17,25},{2,10},{10,18},{18,26},{... | collective-permute-start | bytes 98312 | tf_op jit(solution)/shard_map/ppermute | solution.py:17
  107.7 4.2 %collective-permute-done.8 = f32[1,16,512]{2,1,0:T(8,128)S(1)} collective-permute-done((f32[1,16,512]{2,1,0:T(8,128)S(1)}, f32[1,16,512]{2,1,0:T(8,128)S(1)}, u32[]{:S(2)}, u32[]{:S(2)}) %collective-permute-start.8) | collective-permute-done | bytes 32800 | tf_op jit(solution)/shard_map/ppermute | solution.py:20
  113.5 3.7 %collective-permute-start.11 = (f32[66,1,512]{2,1,0:T(1,128)S(1)}, f32[66,1,512]{2,1,0:T(1,128)S(1)}, u32[]{:S(2)}, u32[]{:S(2)}) collective-permute-start(f32[66,1,512]{2,1,0:T(1,128)S(1)} %get-tuple-element.32), channel_id=1, source_target_pairs={{0,1},{1,2},{2,3},{3,4},{4,5},{5,6},{6,7},{8,9},{9,10},{10,11},{11... | collective-permute-start | bytes 405512 | tf_op jit(solution)/shard_map/ppermute | solution.py:17
  118.2 5.8 %multiply_reduce_fusion.2 = (f32[]{:T(128)}, f32[]{:T(128)}, f32[64,16,512]{2,1,0:T(8,128)}) fusion(f32[64,16,512]{2,1,0:T(8,128)S(1)} %fusion.32, f32[64,16,512]{2,1,0:T(8,128)S(1)} %copy-done.7, f32[64,16,511]{2,1,0:T(8,128)S(1)} %get-tuple-element.46, f32[64,16,511]{2,1,0:T(8,128)S(1)} %get-tuple-element.45, ...), kind=kLoop, calls=%fused_computation.109 | loop fusion | flops 10485758 | bytes 15007752 | tf_op jit(solution)/shard_map/reduce_sum | solution.py:98
  123.9 45.4 %all-reduce.13 = (f32[]{:T(128)}, f32[]{:T(128)}) all-reduce(f32[]{:T(128)} %get-tuple-element.5, f32[]{:T(128)} %get-tuple-element.4), channel_id=1, replica_groups=mesh['gx'=4,'gz'=8] {'gx','gz'}, use_global_device_ids=true, to_apply=%region_2.3 | all-reduce | flops 2 | bytes 16 | tf_op jit(solution)/shard_map/psum | solution.py:97
  170.6 3.6 %fusion.59 = (f32[64,16,512]{2,1,0:T(8,128)S(1)}, f32[64,16,512]{2,1,0:T(8,128)S(1)}) fusion(f32[64,16,512]{2,1,0:T(8,128)} %copy-done.2, f32[64,16,512]{2,1,0:T(8,128)} %get-tuple-element.16, f32[64,16,512]{2,1,0:T(8,128)} %get-tuple-element.13, f32[]{:T(128)S(6)} %div.44), kind=kLoop, calls=%fused_computation.117 | loop fusion | flops 2097152 | bytes 10485764 | tf_op jit(solution)/shard_map/mul | solution.py:86
  174.2 4.2 %collective-permute-start.13 = (f32[1,16,512]{2,1,0:T(8,128)S(1)}, f32[1,16,512]{2,1,0:T(8,128)S(1)}, u32[]{:S(2)}, u32[]{:S(2)}) collective-permute-start(f32[1,16,512]{2,1,0:T(8,128)S(1)} %get-tuple-element.41), channel_id=1, source_target_pairs={{0,8},{8,16},{16,24},{1,9},{9,17},{17,25},{2,10},{10,18},{18,26},{... | collective-permute-start | bytes 98312 | tf_op jit(solution)/shard_map/ppermute | solution.py:17
  180.0 4.2 %collective-permute-done.12 = f32[1,16,512]{2,1,0:T(8,128)S(1)} collective-permute-done((f32[1,16,512]{2,1,0:T(8,128)S(1)}, f32[1,16,512]{2,1,0:T(8,128)S(1)}, u32[]{:S(2)}, u32[]{:S(2)}) %collective-permute-start.12) | collective-permute-done | bytes 32800 | tf_op jit(solution)/shard_map/ppermute | solution.py:20
  185.8 3.2 %collective-permute-start.15 = (f32[66,1,512]{2,1,0:T(1,128)S(1)}, f32[66,1,512]{2,1,0:T(1,128)S(1)}, u32[]{:S(2)}, u32[]{:S(2)}) collective-permute-start(f32[66,1,512]{2,1,0:T(1,128)S(1)} %get-tuple-element.30), channel_id=1, source_target_pairs={{0,1},{1,2},{2,3},{3,4},{4,5},{5,6},{6,7},{8,9},{9,10},{10,11},{11... | collective-permute-start | bytes 405512 | tf_op jit(solution)/shard_map/ppermute | solution.py:17
  190.0 4.2 %fusion.15 = f32[64,16,512]{2,1,0:T(8,128)S(1)} fusion(f32[64,16,512]{2,1,0:T(8,128)S(1)} %get-tuple-element.11, f32[64,16,512]{2,1,0:T(8,128)S(1)} %get-tuple-element.12, f32[66,1,512]{2,1,0:T(1,128)S(1)} %collective-permute-done.15, f32[1,16,512]{2,1,0:T(8,128)S(1)} %collective-permute-done.12, f32[1,16,512]{2,1,0:T(8,128)S(1)} %collective-permute-done.13, ...), kind=kLoop, calls=%fused_computation.29 | loop fusion | flops 10485760 | bytes 15007744 | tf_op jit(solution)/shard_map/add | solution.py:87
  194.2 4.5 %collective-permute-start.17 = (f32[1,16,512]{2,1,0:T(8,128)S(1)}, f32[1,16,512]{2,1,0:T(8,128)S(1)}, u32[]{:S(2)}, u32[]{:S(2)}) collective-permute-start(f32[1,16,512]{2,1,0:T(8,128)S(1)} %get-tuple-element.35), channel_id=1, source_target_pairs={{0,8},{8,16},{16,24},{1,9},{9,17},{17,25},{2,10},{10,18},{18,26},{... | collective-permute-start | bytes 98312 | tf_op jit(solution)/shard_map/ppermute | solution.py:17
  200.3 4.2 %collective-permute-done.16 = f32[1,16,512]{2,1,0:T(8,128)S(1)} collective-permute-done((f32[1,16,512]{2,1,0:T(8,128)S(1)}, f32[1,16,512]{2,1,0:T(8,128)S(1)}, u32[]{:S(2)}, u32[]{:S(2)}) %collective-permute-start.16) | collective-permute-done | bytes 32800 | tf_op jit(solution)/shard_map/ppermute | solution.py:20
  206.1 3.4 %collective-permute-start.19 = (f32[66,1,512]{2,1,0:T(1,128)S(1)}, f32[66,1,512]{2,1,0:T(1,128)S(1)}, u32[]{:S(2)}, u32[]{:S(2)}) collective-permute-start(f32[66,1,512]{2,1,0:T(1,128)S(1)} %get-tuple-element.28), channel_id=1, source_target_pairs={{0,1},{1,2},{2,3},{3,4},{4,5},{5,6},{6,7},{8,9},{9,10},{10,11},{11... | collective-permute-start | bytes 405512 | tf_op jit(solution)/shard_map/ppermute | solution.py:17
  210.4 5.8 %multiply_reduce_fusion = (f32[]{:T(128)}, f32[]{:T(128)}, f32[64,16,512]{2,1,0:T(8,128)}) fusion(f32[64,16,512]{2,1,0:T(8,128)S(1)} %fusion.15, f32[64,16,512]{2,1,0:T(8,128)S(1)} %get-tuple-element.12, f32[64,16,511]{2,1,0:T(8,128)S(1)} %get-tuple-element.38, f32[64,16,511]{2,1,0:T(8,128)S(1)} %get-tuple-element.37, ...), kind=kLoop, calls=%fused_computation.106 | loop fusion | flops 10485758 | bytes 15007752 | tf_op jit(solution)/shard_map/reduce_sum | solution.py:98
  216.3 45.0 %all-reduce.12 = (f32[]{:T(128)}, f32[]{:T(128)}) all-reduce(f32[]{:T(128)} %get-tuple-element.3, f32[]{:T(128)} %get-tuple-element.2), channel_id=1, replica_groups=mesh['gx'=4,'gz'=8] {'gx','gz'}, use_global_device_ids=true, to_apply=%region_6.7 | all-reduce | flops 2 | bytes 16 | tf_op jit(solution)/shard_map/psum | solution.py:97
  265.5 4.4 %multiply_add_fusion = f32[64,16,512]{2,1,0:T(8,128)} fusion(f32[64,16,512]{2,1,0:T(8,128)} %copy-done.1, f32[64,16,512]{2,1,0:T(8,128)} %copy-done, f32[]{:T(128)S(6)} %div.45, f32[]{:T(128)S(6)} %div.47, f32[]{:T(128)S(6)} %div.44), kind=kLoop, calls=%fused_computation.105 | loop fusion | flops 2621440 | bytes 6291468 | tf_op jit(solution)/shard_map/add | solution.py:104
  270.0 2.1 multiply_subtract_fusion
  (61 shorter events, 22.7 us)
Async XLA Ops:
  41.4 6.8 %collective-permute-start = (f32[2,1,16,512]{3,2,1,0:T(8,128)S(1)}, f32[2,1,16,512]{3,2,1,0:T(8,128)S(1)}, u32[]{:S(2)}, u32[]{:S(2)}) collective-permute-start(f32[2,1,16,512]{3,2,1,0:T(8,128)S(1)} %get-tuple-element.21), channel_id=1, source_target_pairs={{0,8},{8,16},{16,24},{1,9},{9,17},{17,25},{2,10},{10,18},{18,26},{... | collective-permute-start | bytes 196616 | tf_op jit(solution)/shard_map/ppermute | solution.py:17
  46.3 6.2 %collective-permute-start.1 = (f32[2,1,16,512]{3,2,1,0:T(8,128)S(1)}, f32[2,1,16,512]{3,2,1,0:T(8,128)S(1)}, u32[]{:S(2)}, u32[]{:S(2)}) collective-permute-start(f32[2,1,16,512]{3,2,1,0:T(8,128)S(1)} %get-tuple-element.22), channel_id=1, source_target_pairs={{8,0},{16,8},{24,16},{9,1},{17,9},{25,17},{10,2},{18,10},{26,18},{... | collective-permute-start | bytes 196616 | tf_op jit(solution)/shard_map/ppermute | solution.py:20
  53.0 2.6 collective-permute-start.2
  54.3 5.2 %collective-permute-start.3 = (f32[2,66,1,512]{3,2,1,0:T(1,128)S(1)}, f32[2,66,1,512]{3,2,1,0:T(1,128)S(1)}, u32[]{:S(2)}, u32[]{:S(2)}) collective-permute-start(f32[2,66,1,512]{3,2,1,0:T(1,128)S(1)} %get-tuple-element.20), channel_id=1, source_target_pairs={{1,0},{2,1},{3,2},{4,3},{5,4},{6,5},{7,6},{9,8},{10,9},{11,10},{12... | collective-permute-start | bytes 811016 | tf_op jit(solution)/shard_map/ppermute | solution.py:20
  76.9 41.3 %copy-start.2 = (f32[64,16,512]{2,1,0:T(8,128)}, f32[64,16,512]{2,1,0:T(8,128)S(1)}, u32[]{:S(2)}) copy-start(f32[64,16,512]{2,1,0:T(8,128)S(1)} %get-tuple-element.15) | copy-start | bytes 6291460
  76.9 20.6 %copy-start.4 = (f32[64,16,512]{2,1,0:T(8,128)S(1)}, f32[64,16,512]{2,1,0:T(8,128)}, u32[]{:S(2)}) copy-start(f32[64,16,512]{2,1,0:T(8,128)} %get-tuple-element.14) | copy-start | bytes 6291460
  77.9 6.0 %collective-permute-start.5 = (f32[1,16,512]{2,1,0:T(8,128)S(1)}, f32[1,16,512]{2,1,0:T(8,128)S(1)}, u32[]{:S(2)}, u32[]{:S(2)}) collective-permute-start(f32[1,16,512]{2,1,0:T(8,128)S(1)} %get-tuple-element.49), channel_id=1, source_target_pairs={{0,8},{8,16},{16,24},{1,9},{9,17},{17,25},{2,10},{10,18},{18,26},{... | collective-permute-start | bytes 98312 | tf_op jit(solution)/shard_map/ppermute | solution.py:17
  82.4 5.8 %collective-permute-start.4 = (f32[1,16,512]{2,1,0:T(8,128)S(1)}, f32[1,16,512]{2,1,0:T(8,128)S(1)}, u32[]{:S(2)}, u32[]{:S(2)}) collective-permute-start(f32[1,16,512]{2,1,0:T(8,128)S(1)} %get-tuple-element.50), channel_id=1, source_target_pairs={{8,0},{16,8},{24,16},{9,1},{17,9},{25,17},{10,2},{18,10},{26,18},{... | collective-permute-start | bytes 98312 | tf_op jit(solution)/shard_map/ppermute | solution.py:20
  90.0 8.4 %collective-permute-start.6 = (f32[66,1,512]{2,1,0:T(1,128)S(1)}, f32[66,1,512]{2,1,0:T(1,128)S(1)}, u32[]{:S(2)}, u32[]{:S(2)}) collective-permute-start(f32[66,1,512]{2,1,0:T(1,128)S(1)} %get-tuple-element.33), channel_id=1, source_target_pairs={{1,0},{2,1},{3,2},{4,3},{5,4},{6,5},{7,6},{9,8},{10,9},{11,10},{12... | collective-permute-start | bytes 405512 | tf_op jit(solution)/shard_map/ppermute | solution.py:20
  91.3 7.1 %copy-start.7 = (f32[64,16,512]{2,1,0:T(8,128)S(1)}, f32[64,16,512]{2,1,0:T(8,128)}, u32[]{:S(2)}) copy-start(f32[64,16,512]{2,1,0:T(8,128)} %get-tuple-element.16) | copy-start | bytes 6291460
  91.3 7.1 %collective-permute-start.7 = (f32[66,1,512]{2,1,0:T(1,128)S(1)}, f32[66,1,512]{2,1,0:T(1,128)S(1)}, u32[]{:S(2)}, u32[]{:S(2)}) collective-permute-start(f32[66,1,512]{2,1,0:T(1,128)S(1)} %get-tuple-element.34), channel_id=1, source_target_pairs={{0,1},{1,2},{2,3},{3,4},{4,5},{5,6},{6,7},{8,9},{9,10},{10,11},{11... | collective-permute-start | bytes 405512 | tf_op jit(solution)/shard_map/ppermute | solution.py:17
  102.7 15.5 %copy-start = (f32[64,16,512]{2,1,0:T(8,128)}, f32[64,16,512]{2,1,0:T(8,128)S(1)}, u32[]{:S(2)}) copy-start(f32[64,16,512]{2,1,0:T(8,128)S(1)} %fusion.32) | copy-start | bytes 6291460
  102.7 5.0 %collective-permute-start.9 = (f32[1,16,512]{2,1,0:T(8,128)S(1)}, f32[1,16,512]{2,1,0:T(8,128)S(1)}, u32[]{:S(2)}, u32[]{:S(2)}) collective-permute-start(f32[1,16,512]{2,1,0:T(8,128)S(1)} %get-tuple-element.43), channel_id=1, source_target_pairs={{0,8},{8,16},{16,24},{1,9},{9,17},{17,25},{2,10},{10,18},{18,26},{... | collective-permute-start | bytes 98312 | tf_op jit(solution)/shard_map/ppermute | solution.py:17
  106.1 5.8 %collective-permute-start.8 = (f32[1,16,512]{2,1,0:T(8,128)S(1)}, f32[1,16,512]{2,1,0:T(8,128)S(1)}, u32[]{:S(2)}, u32[]{:S(2)}) collective-permute-start(f32[1,16,512]{2,1,0:T(8,128)S(1)} %get-tuple-element.44), channel_id=1, source_target_pairs={{8,0},{16,8},{24,16},{9,1},{17,9},{25,17},{10,2},{18,10},{26,18},{... | collective-permute-start | bytes 98312 | tf_op jit(solution)/shard_map/ppermute | solution.py:20
  112.2 5.9 %collective-permute-start.10 = (f32[66,1,512]{2,1,0:T(1,128)S(1)}, f32[66,1,512]{2,1,0:T(1,128)S(1)}, u32[]{:S(2)}, u32[]{:S(2)}) collective-permute-start(f32[66,1,512]{2,1,0:T(1,128)S(1)} %get-tuple-element.31), channel_id=1, source_target_pairs={{1,0},{2,1},{3,2},{4,3},{5,4},{6,5},{7,6},{9,8},{10,9},{11,10},{12... | collective-permute-start | bytes 405512 | tf_op jit(solution)/shard_map/ppermute | solution.py:20
  113.5 4.7 %collective-permute-start.11 = (f32[66,1,512]{2,1,0:T(1,128)S(1)}, f32[66,1,512]{2,1,0:T(1,128)S(1)}, u32[]{:S(2)}, u32[]{:S(2)}) collective-permute-start(f32[66,1,512]{2,1,0:T(1,128)S(1)} %get-tuple-element.32), channel_id=1, source_target_pairs={{0,1},{1,2},{2,3},{3,4},{4,5},{5,6},{6,7},{8,9},{9,10},{10,11},{11... | collective-permute-start | bytes 405512 | tf_op jit(solution)/shard_map/ppermute | solution.py:17
  174.2 36.2 %copy-start.5 = (f32[64,16,512]{2,1,0:T(8,128)}, f32[64,16,512]{2,1,0:T(8,128)S(1)}, u32[]{:S(2)}) copy-start(f32[64,16,512]{2,1,0:T(8,128)S(1)} %get-tuple-element.12) | copy-start | bytes 6291460
  174.2 5.8 %collective-permute-start.13 = (f32[1,16,512]{2,1,0:T(8,128)S(1)}, f32[1,16,512]{2,1,0:T(8,128)S(1)}, u32[]{:S(2)}, u32[]{:S(2)}) collective-permute-start(f32[1,16,512]{2,1,0:T(8,128)S(1)} %get-tuple-element.41), channel_id=1, source_target_pairs={{0,8},{8,16},{16,24},{1,9},{9,17},{17,25},{2,10},{10,18},{18,26},{... | collective-permute-start | bytes 98312 | tf_op jit(solution)/shard_map/ppermute | solution.py:17
  178.4 5.8 %collective-permute-start.12 = (f32[1,16,512]{2,1,0:T(8,128)S(1)}, f32[1,16,512]{2,1,0:T(8,128)S(1)}, u32[]{:S(2)}, u32[]{:S(2)}) collective-permute-start(f32[1,16,512]{2,1,0:T(8,128)S(1)} %get-tuple-element.42), channel_id=1, source_target_pairs={{8,0},{16,8},{24,16},{9,1},{17,9},{25,17},{10,2},{18,10},{26,18},{... | collective-permute-start | bytes 98312 | tf_op jit(solution)/shard_map/ppermute | solution.py:20
  184.5 5.3 %collective-permute-start.14 = (f32[66,1,512]{2,1,0:T(1,128)S(1)}, f32[66,1,512]{2,1,0:T(1,128)S(1)}, u32[]{:S(2)}, u32[]{:S(2)}) collective-permute-start(f32[66,1,512]{2,1,0:T(1,128)S(1)} %get-tuple-element.29), channel_id=1, source_target_pairs={{1,0},{2,1},{3,2},{4,3},{5,4},{6,5},{7,6},{9,8},{10,9},{11,10},{12... | collective-permute-start | bytes 405512 | tf_op jit(solution)/shard_map/ppermute | solution.py:20
  185.8 4.2 %copy-start.3 = (f32[64,16,512]{2,1,0:T(8,128)S(1)}, f32[64,16,512]{2,1,0:T(8,128)}, u32[]{:S(2)}) copy-start(f32[64,16,512]{2,1,0:T(8,128)} %copy-done.2) | copy-start | bytes 6291460
  185.8 4.1 %collective-permute-start.15 = (f32[66,1,512]{2,1,0:T(1,128)S(1)}, f32[66,1,512]{2,1,0:T(1,128)S(1)}, u32[]{:S(2)}, u32[]{:S(2)}) collective-permute-start(f32[66,1,512]{2,1,0:T(1,128)S(1)} %get-tuple-element.30), channel_id=1, source_target_pairs={{0,1},{1,2},{2,3},{3,4},{4,5},{5,6},{6,7},{8,9},{9,10},{10,11},{11... | collective-permute-start | bytes 405512 | tf_op jit(solution)/shard_map/ppermute | solution.py:17
  194.2 16.2 %copy-start.1 = (f32[64,16,512]{2,1,0:T(8,128)}, f32[64,16,512]{2,1,0:T(8,128)S(1)}, u32[]{:S(2)}) copy-start(f32[64,16,512]{2,1,0:T(8,128)S(1)} %fusion.15) | copy-start | bytes 6291460
  194.2 6.1 %collective-permute-start.17 = (f32[1,16,512]{2,1,0:T(8,128)S(1)}, f32[1,16,512]{2,1,0:T(8,128)S(1)}, u32[]{:S(2)}, u32[]{:S(2)}) collective-permute-start(f32[1,16,512]{2,1,0:T(8,128)S(1)} %get-tuple-element.35), channel_id=1, source_target_pairs={{0,8},{8,16},{16,24},{1,9},{9,17},{17,25},{2,10},{10,18},{18,26},{... | collective-permute-start | bytes 98312 | tf_op jit(solution)/shard_map/ppermute | solution.py:17
  198.7 5.8 %collective-permute-start.16 = (f32[1,16,512]{2,1,0:T(8,128)S(1)}, f32[1,16,512]{2,1,0:T(8,128)S(1)}, u32[]{:S(2)}, u32[]{:S(2)}) collective-permute-start(f32[1,16,512]{2,1,0:T(8,128)S(1)} %get-tuple-element.36), channel_id=1, source_target_pairs={{8,0},{16,8},{24,16},{9,1},{17,9},{25,17},{10,2},{18,10},{26,18},{... | collective-permute-start | bytes 98312 | tf_op jit(solution)/shard_map/ppermute | solution.py:20
  204.8 5.6 %collective-permute-start.18 = (f32[66,1,512]{2,1,0:T(1,128)S(1)}, f32[66,1,512]{2,1,0:T(1,128)S(1)}, u32[]{:S(2)}, u32[]{:S(2)}) collective-permute-start(f32[66,1,512]{2,1,0:T(1,128)S(1)} %get-tuple-element.27), channel_id=1, source_target_pairs={{1,0},{2,1},{3,2},{4,3},{5,4},{6,5},{7,6},{9,8},{10,9},{11,10},{12... | collective-permute-start | bytes 405512 | tf_op jit(solution)/shard_map/ppermute | solution.py:20
  206.1 4.3 %collective-permute-start.19 = (f32[66,1,512]{2,1,0:T(1,128)S(1)}, f32[66,1,512]{2,1,0:T(1,128)S(1)}, u32[]{:S(2)}, u32[]{:S(2)}) collective-permute-start(f32[66,1,512]{2,1,0:T(1,128)S(1)} %get-tuple-element.28), channel_id=1, source_target_pairs={{0,1},{1,2},{2,3},{3,4},{4,5},{5,6},{6,7},{8,9},{9,10},{10,11},{11... | collective-permute-start | bytes 405512 | tf_op jit(solution)/shard_map/ppermute | solution.py:17
  265.5 4.5 %copy-start.6 = (f32[64,16,512]{2,1,0:T(8,128)S(1)}, f32[64,16,512]{2,1,0:T(8,128)}, u32[]{:S(2)}) copy-start(f32[64,16,512]{2,1,0:T(8,128)} %copy-done.5) | copy-start | bytes 6291460
  265.5 4.4 %copy-start.8 = (f32[64,16,512]{2,1,0:T(8,128)S(1)}, f32[64,16,512]{2,1,0:T(8,128)}, u32[]{:S(2)}) copy-start(f32[64,16,512]{2,1,0:T(8,128)} %get-tuple-element.13) | copy-start | bytes 6291460
  265.5 4.4 %copy-start.9 = (f32[64,16,512]{2,1,0:T(8,128)S(1)}, f32[64,16,512]{2,1,0:T(8,128)}, u32[]{:S(2)}) copy-start(f32[64,16,512]{2,1,0:T(8,128)} %get-tuple-element.10) | copy-start | bytes 6291460
where the time goes:
time: 273 us; the launch traced here: 272 us
  blocking collectives  90.4 us (33%)
  starting transfers between devices  52.2 us (19%)
  other arithmetic  48.8 us (18%)
  local copies, waits for them, and re-layouts  47 us (17%)
  waiting for transfers between devices  27.1 us (10%)
  between operations  6.58 us (2%)
    psum x2, blocking collectives, both_sums(): lax.psum((jnp.sum(current * preconditioned), jnp.sum(image_of * precondit...  90.4 us
    ppermute x10, starting transfers between devices, with_halo(): lax.ppermute(lax.slice_in_dim(block, block.shape[dim] - width, None, axis...  39.3 us
    ppermute x10, waiting for transfers between devices, with_halo(): lax.ppermute(lax.slice_in_dim(block, 0, width, axis=dim), axis, backward)  25.1 us
    reshape x1, local copies, waits for them, and re-layouts, on_device(): active = jnp.broadcast_to(listed_hit[:, None, :, None, :, None], (tiles_x...  25.1 us
    ppermute x10, starting transfers between devices, with_halo(): lax.ppermute(lax.slice_in_dim(block, 0, width, axis=dim), axis, backward)  12.9 us
    mul x2, other arithmetic, precondition(): first_pass = scale_mid * residual  12.3 us
    reduce_sum x2, other arithmetic, both_sums(): jnp.sum(image_of * preconditioned)  11.6 us
    broadcast_in_dim x1, local copies, waits for them, and re-layouts, on_device(): jnp.broadcast_to(listed_hit[:, None, :, None, :, None], (tiles_x, TILE, t...  11.3 us
  transfers between devices with their start and end apart: 20, of which 13 were waited for; matrix products, arithmetic and copies ran while one was open for 1% of the time, Pallas kernels for 0%

commit v1 on v0

--- a/solution.py
+++ b/solution.py
@@ -95,7 +95,8 @@
 
     def both_sums(current, preconditioned, image_of):
         return lax.psum(
-            (jnp.sum(current * preconditioned), jnp.sum(image_of * preconditioned)), ("gx", "gz")
+            lax.psum((jnp.sum(current * preconditioned), jnp.sum(image_of * preconditioned)), "gz"),
+            "gx",
         )
 
     gamma_now, delta_now = both_sums(residual, smoothed, precond_image)

time: 273 us -> 239 us (0.88)
  blocking collectives: 90.4 us -> 56.6 us
    psum x2, blocking collectives: 90.4 us -> 38.5 us  [both_sums(): lax.psum((jnp.sum(current * preconditioned), jnp.sum(image_of * precondit...]
    psum x0 -> x2, blocking collectives: none -> 18.1 us  [both_sums(): lax.psum(lax.psum((jnp.sum(current * preconditioned), jnp.sum(image_of *...]
where the time goes in v1:
time: 239 us; the launch traced here: 237 us
  blocking collectives  56.6 us (24%)
  starting transfers between devices  51 us (21%)
  other arithmetic  48.7 us (20%)
  local copies, waits for them, and re-layouts  47 us (20%)
  waiting for transfers between devices  27.2 us (11%)
  between operations  6.8 us (3%)
    psum x2, blocking collectives, both_sums(): lax.psum((jnp.sum(current * preconditioned), jnp.sum(image_of * precondit...  38.5 us
    ppermute x10, starting transfers between devices, with_halo(): lax.ppermute(lax.slice_in_dim(block, block.shape[dim] - width, None, axis...  38 us
    ppermute x10, waiting for transfers between devices, with_halo(): lax.ppermute(lax.slice_in_dim(block, 0, width, axis=dim), axis, backward)  25.1 us
    reshape x1, local copies, waits for them, and re-layouts, on_device(): active = jnp.broadcast_to(listed_hit[:, None, :, None, :, None], (tiles_x...  25.1 us
    psum x2, blocking collectives, both_sums(): lax.psum(lax.psum((jnp.sum(current * preconditioned), jnp.sum(image_of *...  18.1 us
    ppermute x10, starting transfers between devices, with_halo(): lax.ppermute(lax.slice_in_dim(block, 0, width, axis=dim), axis, backward)  12.9 us
    mul x2, other arithmetic, precondition(): first_pass = scale_mid * residual  12.3 us
    reduce_sum x2, other arithmetic, both_sums(): jnp.sum(image_of * preconditioned)  11.5 us
  transfers between devices with their start and end apart: 20, of which 13 were waited for; matrix products, arithmetic and copies ran while one was open for 1% of the time, Pallas kernels for 0%

profile of v1, /device:TPU:0, one launch (start us, length us, event | category | flops | bytes accessed | tf_op | source)
XLA Modules:
  0.0 237.3 jit_solution(8926655003821821242)
XLA Ops:
  2.0 11.3 %broadcast_in_dim.18 = f32[8,8,2,8,64,8]{5,4,3,2,1,0:T(8,128)} broadcast(f32[8,2,64]{2,1,0:T(2,128)S(1)} %reshape.16), dimensions={0,2,4} | broadcast | bytes 2101248 | tf_op jit(solution)/shard_map/broadcast_in_dim | solution.py:71
  13.4 25.1 %reshape.15 = f32[64,16,512]{2,1,0:T(8,128)} reshape(f32[8,8,2,8,64,8]{5,4,3,2,1,0:T(8,128)} %broadcast_in_dim.18) | data formatting | bytes 4194304 | tf_op jit(solution)/shard_map/reshape | solution.py:73
  38.4 3.0 %abs_bitcast_fusion = (f32[1,64,16,512]{3,2,1,0:T(8,128)S(1)}, f32[1,64,16,512]{3,2,1,0:T(8,128)S(1)}) fusion(f32[64,16,512]{2,1,0:T(8,128)} %param.4, f32[64,16,512]{2,1,0:T(8,128)} %reshape.15), kind=kLoop, calls=%fused_computation.114 | loop fusion | flops 1572864 | bytes 8388608 | tf_op jit(solution)/shard_map/stack | solution.py:76
  41.4 4.9 %collective-permute-start = (f32[2,1,16,512]{3,2,1,0:T(8,128)S(1)}, f32[2,1,16,512]{3,2,1,0:T(8,128)S(1)}, u32[]{:S(2)}, u32[]{:S(2)}) collective-permute-start(f32[2,1,16,512]{3,2,1,0:T(8,128)S(1)} %get-tuple-element.25), channel_id=1, source_target_pairs={{0,8},{8,16},{16,24},{1,9},{9,17},{17,25},{2,10},{10,18},{18,26},{... | collective-permute-start | bytes 196616 | tf_op jit(solution)/shard_map/ppermute | solution.py:17
  48.2 4.3 %collective-permute-done.1 = f32[2,1,16,512]{3,2,1,0:T(8,128)S(1)} collective-permute-done((f32[2,1,16,512]{3,2,1,0:T(8,128)S(1)}, f32[2,1,16,512]{3,2,1,0:T(8,128)S(1)}, u32[]{:S(2)}, u32[]{:S(2)}) %collective-permute-start.1) | collective-permute-done | bytes 65568 | tf_op jit(solution)/shard_map/ppermute | solution.py:20
  55.6 3.9 %collective-permute-done.3 = f32[2,66,1,512]{3,2,1,0:T(1,128)S(1)} collective-permute-done((f32[2,66,1,512]{3,2,1,0:T(1,128)S(1)}, f32[2,66,1,512]{3,2,1,0:T(1,128)S(1)}, u32[]{:S(2)}, u32[]{:S(2)}) %collective-permute-start.3) | collective-permute-done | bytes 270368 | tf_op jit(solution)/shard_map/ppermute | solution.py:20
  59.6 2.5 %pad_maximum_fusion = f32[2,66,18,512]{3,2,1,0:T(8,128)S(1)} fusion(f32[2,66,1,512]{3,2,1,0:T(1,128)S(1)} %collective-permute-done.3, f32[2,1,16,512]{3,2,1,0:T(8,128)S(1)} %collective-permute-done.1, f32[1,64,16,512]{3,2,1,0:T(8,128)S(1)} %get-tuple-element.56, f32[1,64,16,512]{3,2,1,0:T(8,128)S(1)} %get-tuple-element.55, ...), kind=kLoop, calls=%fused_computation | loop fusion | flops 6082560 | bytes 9732096 | tf_op jit(solution)/shard_map/concatenate | solution.py:21
  62.8 5.4 %fusion.64 = (f32[64,16,511]{2,1,0:T(8,128)}, f32[64,16,511]{2,1,0:T(8,128)}, f32[64,16,511]{2,1,0:T(8,128)}, f32[64,16,511]{2,1,0:T(8,128)}) fusion(f32[66,18,512]{2,1,0:T(8,128)S(1)} %get-tuple-element.21, f32[66,18,512]{2,1,0:T(8,128)S(1)} %get-tuple-element.22), kind=kLoop, calls=%fused_computation.137 | loop fusion | bytes 16744448 | tf_op jit(solution)/shard_map/slice | solution.py:27
  68.2 8.7 %fusion.60 = (f32[64,16,512]{2,1,0:T(8,128)}, f32[64,16,512]{2,1,0:T(8,128)S(1)}, f32[64,16,512]{2,1,0:T(8,128)}) fusion(f32[64,16,511]{2,1,0:T(8,128)} %get-tuple-element.57, f32[64,16,511]{2,1,0:T(8,128)} %get-tuple-element.28, f32[64,16,511]{2,1,0:T(8,128)} %get-tuple-element.58, f32[64,16,511]{2,1,0:T(8,128)} %get-tuple-element.27, ...), kind=kLoop, calls=%fused_computation.118 | loop fusion | flops 22020096 | bytes 37732352 | tf_op jit(solution)/shard_map/mul | solution.py:86
  77.9 4.4 %collective-permute-start.5 = (f32[1,16,512]{2,1,0:T(8,128)S(1)}, f32[1,16,512]{2,1,0:T(8,128)S(1)}, u32[]{:S(2)}, u32[]{:S(2)}) collective-permute-start(f32[1,16,512]{2,1,0:T(8,128)S(1)} %get-tuple-element.53), channel_id=1, source_target_pairs={{0,8},{8,16},{16,24},{1,9},{9,17},{17,25},{2,10},{10,18},{18,26},{... | collective-permute-start | bytes 98312 | tf_op jit(solution)/shard_map/ppermute | solution.py:17
  83.9 4.2 %collective-permute-done.4 = f32[1,16,512]{2,1,0:T(8,128)S(1)} collective-permute-done((f32[1,16,512]{2,1,0:T(8,128)S(1)}, f32[1,16,512]{2,1,0:T(8,128)S(1)}, u32[]{:S(2)}, u32[]{:S(2)}) %collective-permute-start.4) | collective-permute-done | bytes 32800 | tf_op jit(solution)/shard_map/ppermute | solution.py:20
  91.3 6.3 %collective-permute-start.7 = (f32[66,1,512]{2,1,0:T(1,128)S(1)}, f32[66,1,512]{2,1,0:T(1,128)S(1)}, u32[]{:S(2)}, u32[]{:S(2)}) collective-permute-start(f32[66,1,512]{2,1,0:T(1,128)S(1)} %get-tuple-element.38), channel_id=1, source_target_pairs={{0,1},{1,2},{2,3},{3,4},{4,5},{5,6},{6,7},{8,9},{9,10},{10,11},{11... | collective-permute-start | bytes 405512 | tf_op jit(solution)/shard_map/ppermute | solution.py:17
  98.4 4.2 %fusion.32 = f32[64,16,512]{2,1,0:T(8,128)S(1)} fusion(f32[64,16,512]{2,1,0:T(8,128)S(1)} %copy-done.4, f32[64,16,512]{2,1,0:T(8,128)S(1)} %copy-done.7, f32[66,1,512]{2,1,0:T(1,128)S(1)} %collective-permute-done.7, f32[1,16,512]{2,1,0:T(8,128)S(1)} %collective-permute-done.4, f32[1,16,512]{2,1,0:T(8,128)S(1)} %collective-permute-done.5, ...), kind=kLoop, calls=%fused_computation.62 | loop fusion | flops 10485760 | bytes 15007744 | tf_op jit(solution)/shard_map/add | solution.py:87
  102.7 3.4 %collective-permute-start.9 = (f32[1,16,512]{2,1,0:T(8,128)S(1)}, f32[1,16,512]{2,1,0:T(8,128)S(1)}, u32[]{:S(2)}, u32[]{:S(2)}) collective-permute-start(f32[1,16,512]{2,1,0:T(8,128)S(1)} %get-tuple-element.47), channel_id=1, source_target_pairs={{0,8},{8,16},{16,24},{1,9},{9,17},{17,25},{2,10},{10,18},{18,26},{... | collective-permute-start | bytes 98312 | tf_op jit(solution)/shard_map/ppermute | solution.py:17
  107.7 4.2 %collective-permute-done.8 = f32[1,16,512]{2,1,0:T(8,128)S(1)} collective-permute-done((f32[1,16,512]{2,1,0:T(8,128)S(1)}, f32[1,16,512]{2,1,0:T(8,128)S(1)}, u32[]{:S(2)}, u32[]{:S(2)}) %collective-permute-start.8) | collective-permute-done | bytes 32800 | tf_op jit(solution)/shard_map/ppermute | solution.py:20
  113.4 3.7 %collective-permute-start.11 = (f32[66,1,512]{2,1,0:T(1,128)S(1)}, f32[66,1,512]{2,1,0:T(1,128)S(1)}, u32[]{:S(2)}, u32[]{:S(2)}) collective-permute-start(f32[66,1,512]{2,1,0:T(1,128)S(1)} %get-tuple-element.36), channel_id=1, source_target_pairs={{0,1},{1,2},{2,3},{3,4},{4,5},{5,6},{6,7},{8,9},{9,10},{10,11},{11... | collective-permute-start | bytes 405512 | tf_op jit(solution)/shard_map/ppermute | solution.py:17
  118.1 5.7 %multiply_reduce_fusion.2 = (f32[]{:T(128)}, f32[]{:T(128)}, f32[64,16,512]{2,1,0:T(8,128)}) fusion(f32[64,16,512]{2,1,0:T(8,128)S(1)} %fusion.32, f32[64,16,512]{2,1,0:T(8,128)S(1)} %copy-done.7, f32[64,16,511]{2,1,0:T(8,128)S(1)} %get-tuple-element.50, f32[64,16,511]{2,1,0:T(8,128)S(1)} %get-tuple-element.49, ...), kind=kLoop, calls=%fused_computation.109 | loop fusion | flops 10485758 | bytes 15007752 | tf_op jit(solution)/shard_map/reduce_sum | solution.py:98
  123.8 20.6 %all-reduce.13 = (f32[]{:T(128)}, f32[]{:T(128)}) all-reduce(f32[]{:T(128)} %get-tuple-element.5, f32[]{:T(128)} %get-tuple-element.4), channel_id=1, replica_groups=mesh['gx'=4,'gz'=8] {'gz'}, use_global_device_ids=true, to_apply=%region_2.3 | all-reduce | flops 2 | bytes 16 | tf_op jit(solution)/shard_map/psum | solution.py:98
  144.4 9.0 %all-reduce.15 = (f32[]{:T(128)}, f32[]{:T(128)}) all-reduce(f32[]{:T(128)} %get-tuple-element.8, f32[]{:T(128)} %get-tuple-element.9), channel_id=1, replica_groups=mesh['gx'=4,'gz'=8] {'gx'}, use_global_device_ids=true, to_apply=%region_3.4 | all-reduce | flops 2 | bytes 16 | tf_op jit(solution)/shard_map/psum | solution.py:97
  154.8 3.6 %fusion.59 = (f32[64,16,512]{2,1,0:T(8,128)S(1)}, f32[64,16,512]{2,1,0:T(8,128)S(1)}) fusion(f32[64,16,512]{2,1,0:T(8,128)} %copy-done.2, f32[64,16,512]{2,1,0:T(8,128)} %get-tuple-element.20, f32[64,16,512]{2,1,0:T(8,128)} %get-tuple-element.17, f32[]{:T(128)S(6)} %div.44), kind=kLoop, calls=%fused_computation.117 | loop fusion | flops 2097152 | bytes 10485764 | tf_op jit(solution)/shard_map/mul | solution.py:86
  158.4 3.0 %collective-permute-start.13 = (f32[1,16,512]{2,1,0:T(8,128)S(1)}, f32[1,16,512]{2,1,0:T(8,128)S(1)}, u32[]{:S(2)}, u32[]{:S(2)}) collective-permute-start(f32[1,16,512]{2,1,0:T(8,128)S(1)} %get-tuple-element.45), channel_id=1, source_target_pairs={{0,8},{8,16},{16,24},{1,9},{9,17},{17,25},{2,10},{10,18},{18,26},{... | collective-permute-start | bytes 98312 | tf_op jit(solution)/shard_map/ppermute | solution.py:17
  163.0 4.2 %collective-permute-done.12 = f32[1,16,512]{2,1,0:T(8,128)S(1)} collective-permute-done((f32[1,16,512]{2,1,0:T(8,128)S(1)}, f32[1,16,512]{2,1,0:T(8,128)S(1)}, u32[]{:S(2)}, u32[]{:S(2)}) %collective-permute-start.12) | collective-permute-done | bytes 32800 | tf_op jit(solution)/shard_map/ppermute | solution.py:20
  168.8 3.2 %collective-permute-start.15 = (f32[66,1,512]{2,1,0:T(1,128)S(1)}, f32[66,1,512]{2,1,0:T(1,128)S(1)}, u32[]{:S(2)}, u32[]{:S(2)}) collective-permute-start(f32[66,1,512]{2,1,0:T(1,128)S(1)} %get-tuple-element.34), channel_id=1, source_target_pairs={{0,1},{1,2},{2,3},{3,4},{4,5},{5,6},{6,7},{8,9},{9,10},{10,11},{11... | collective-permute-start | bytes 405512 | tf_op jit(solution)/shard_map/ppermute | solution.py:17
  172.9 4.2 %fusion.15 = f32[64,16,512]{2,1,0:T(8,128)S(1)} fusion(f32[64,16,512]{2,1,0:T(8,128)S(1)} %get-tuple-element.15, f32[64,16,512]{2,1,0:T(8,128)S(1)} %get-tuple-element.16, f32[66,1,512]{2,1,0:T(1,128)S(1)} %collective-permute-done.15, f32[1,16,512]{2,1,0:T(8,128)S(1)} %collective-permute-done.12, f32[1,16,512]{2,1,0:T(8,128)S(1)} %collective-permute-done.13, ...), kind=kLoop, calls=%fused_computation.29 | loop fusion | flops 10485760 | bytes 15007744 | tf_op jit(solution)/shard_map/add | solution.py:87
  177.2 4.7 %collective-permute-start.17 = (f32[1,16,512]{2,1,0:T(8,128)S(1)}, f32[1,16,512]{2,1,0:T(8,128)S(1)}, u32[]{:S(2)}, u32[]{:S(2)}) collective-permute-start(f32[1,16,512]{2,1,0:T(8,128)S(1)} %get-tuple-element.39), channel_id=1, source_target_pairs={{0,8},{8,16},{16,24},{1,9},{9,17},{17,25},{2,10},{10,18},{18,26},{... | collective-permute-start | bytes 98312 | tf_op jit(solution)/shard_map/ppermute | solution.py:17
  183.6 4.2 %collective-permute-done.16 = f32[1,16,512]{2,1,0:T(8,128)S(1)} collective-permute-done((f32[1,16,512]{2,1,0:T(8,128)S(1)}, f32[1,16,512]{2,1,0:T(8,128)S(1)}, u32[]{:S(2)}, u32[]{:S(2)}) %collective-permute-start.16) | collective-permute-done | bytes 32800 | tf_op jit(solution)/shard_map/ppermute | solution.py:20
  189.3 3.3 %collective-permute-start.19 = (f32[66,1,512]{2,1,0:T(1,128)S(1)}, f32[66,1,512]{2,1,0:T(1,128)S(1)}, u32[]{:S(2)}, u32[]{:S(2)}) collective-permute-start(f32[66,1,512]{2,1,0:T(1,128)S(1)} %get-tuple-element.32), channel_id=1, source_target_pairs={{0,1},{1,2},{2,3},{3,4},{4,5},{5,6},{6,7},{8,9},{9,10},{10,11},{11... | collective-permute-start | bytes 405512 | tf_op jit(solution)/shard_map/ppermute | solution.py:17
  193.5 5.8 %multiply_reduce_fusion = (f32[]{:T(128)}, f32[]{:T(128)}, f32[64,16,512]{2,1,0:T(8,128)}) fusion(f32[64,16,512]{2,1,0:T(8,128)S(1)} %fusion.15, f32[64,16,512]{2,1,0:T(8,128)S(1)} %get-tuple-element.16, f32[64,16,511]{2,1,0:T(8,128)S(1)} %get-tuple-element.42, f32[64,16,511]{2,1,0:T(8,128)S(1)} %get-tuple-element.41, ...), kind=kLoop, calls=%fused_computation.106 | loop fusion | flops 10485758 | bytes 15007752 | tf_op jit(solution)/shard_map/reduce_sum | solution.py:98
  199.3 18.0 %all-reduce.12 = (f32[]{:T(128)}, f32[]{:T(128)}) all-reduce(f32[]{:T(128)} %get-tuple-element.3, f32[]{:T(128)} %get-tuple-element.2), channel_id=1, replica_groups=mesh['gx'=4,'gz'=8] {'gz'}, use_global_device_ids=true, to_apply=%region_8.9 | all-reduce | flops 2 | bytes 16 | tf_op jit(solution)/shard_map/psum | solution.py:98
  217.3 9.0 %all-reduce.14 = (f32[]{:T(128)}, f32[]{:T(128)}) all-reduce(f32[]{:T(128)} %get-tuple-element.6, f32[]{:T(128)} %get-tuple-element.7), channel_id=1, replica_groups=mesh['gx'=4,'gz'=8] {'gx'}, use_global_device_ids=true, to_apply=%region_9.10 | all-reduce | flops 2 | bytes 16 | tf_op jit(solution)/shard_map/psum | solution.py:97
  230.7 4.4 %multiply_add_fusion = f32[64,16,512]{2,1,0:T(8,128)} fusion(f32[64,16,512]{2,1,0:T(8,128)} %copy-done.1, f32[64,16,512]{2,1,0:T(8,128)} %copy-done, f32[]{:T(128)S(6)} %div.45, f32[]{:T(128)S(6)} %div.47, f32[]{:T(128)S(6)} %div.44), kind=kLoop, calls=%fused_computation.105 | loop fusion | flops 2621440 | bytes 6291468 | tf_op jit(solution)/shard_map/add | solution.py:105
  235.2 2.1 multiply_subtract_fusion
  (63 shorter events, 26.0 us)
Async XLA Ops:
  41.4 6.8 %collective-permute-start = (f32[2,1,16,512]{3,2,1,0:T(8,128)S(1)}, f32[2,1,16,512]{3,2,1,0:T(8,128)S(1)}, u32[]{:S(2)}, u32[]{:S(2)}) collective-permute-start(f32[2,1,16,512]{3,2,1,0:T(8,128)S(1)} %get-tuple-element.25), channel_id=1, source_target_pairs={{0,8},{8,16},{16,24},{1,9},{9,17},{17,25},{2,10},{10,18},{18,26},{... | collective-permute-start | bytes 196616 | tf_op jit(solution)/shard_map/ppermute | solution.py:17
  46.3 6.2 %collective-permute-start.1 = (f32[2,1,16,512]{3,2,1,0:T(8,128)S(1)}, f32[2,1,16,512]{3,2,1,0:T(8,128)S(1)}, u32[]{:S(2)}, u32[]{:S(2)}) collective-permute-start(f32[2,1,16,512]{3,2,1,0:T(8,128)S(1)} %get-tuple-element.26), channel_id=1, source_target_pairs={{8,0},{16,8},{24,16},{9,1},{17,9},{25,17},{10,2},{18,10},{26,18},{... | collective-permute-start | bytes 196616 | tf_op jit(solution)/shard_map/ppermute | solution.py:20
  53.0 2.6 %collective-permute-start.2 = (f32[2,66,1,512]{3,2,1,0:T(1,128)S(1)}, f32[2,66,1,512]{3,2,1,0:T(1,128)S(1)}, u32[]{:S(2)}, u32[]{:S(2)}) collective-permute-start(f32[2,66,1,512]{3,2,1,0:T(1,128)S(1)} %get-tuple-element.23), channel_id=1, source_target_pairs={{0,1},{1,2},{2,3},{3,4},{4,5},{5,6},{6,7},{8,9},{9,10},{10,11},{11... | collective-permute-start | bytes 811016 | tf_op jit(solution)/shard_map/ppermute | solution.py:17
  54.3 5.2 %collective-permute-start.3 = (f32[2,66,1,512]{3,2,1,0:T(1,128)S(1)}, f32[2,66,1,512]{3,2,1,0:T(1,128)S(1)}, u32[]{:S(2)}, u32[]{:S(2)}) collective-permute-start(f32[2,66,1,512]{3,2,1,0:T(1,128)S(1)} %get-tuple-element.24), channel_id=1, source_target_pairs={{1,0},{2,1},{3,2},{4,3},{5,4},{6,5},{7,6},{9,8},{10,9},{11,10},{12... | collective-permute-start | bytes 811016 | tf_op jit(solution)/shard_map/ppermute | solution.py:20
  76.9 41.3 %copy-start.2 = (f32[64,16,512]{2,1,0:T(8,128)}, f32[64,16,512]{2,1,0:T(8,128)S(1)}, u32[]{:S(2)}) copy-start(f32[64,16,512]{2,1,0:T(8,128)S(1)} %get-tuple-element.19) | copy-start | bytes 6291460
  76.9 20.6 %copy-start.4 = (f32[64,16,512]{2,1,0:T(8,128)S(1)}, f32[64,16,512]{2,1,0:T(8,128)}, u32[]{:S(2)}) copy-start(f32[64,16,512]{2,1,0:T(8,128)} %get-tuple-element.18) | copy-start | bytes 6291460
  77.9 6.0 %collective-permute-start.5 = (f32[1,16,512]{2,1,0:T(8,128)S(1)}, f32[1,16,512]{2,1,0:T(8,128)S(1)}, u32[]{:S(2)}, u32[]{:S(2)}) collective-permute-start(f32[1,16,512]{2,1,0:T(8,128)S(1)} %get-tuple-element.53), channel_id=1, source_target_pairs={{0,8},{8,16},{16,24},{1,9},{9,17},{17,25},{2,10},{10,18},{18,26},{... | collective-permute-start | bytes 98312 | tf_op jit(solution)/shard_map/ppermute | solution.py:17
  82.3 5.8 %collective-permute-start.4 = (f32[1,16,512]{2,1,0:T(8,128)S(1)}, f32[1,16,512]{2,1,0:T(8,128)S(1)}, u32[]{:S(2)}, u32[]{:S(2)}) collective-permute-start(f32[1,16,512]{2,1,0:T(8,128)S(1)} %get-tuple-element.54), channel_id=1, source_target_pairs={{8,0},{16,8},{24,16},{9,1},{17,9},{25,17},{10,2},{18,10},{26,18},{... | collective-permute-start | bytes 98312 | tf_op jit(solution)/shard_map/ppermute | solution.py:20
  90.0 8.4 %collective-permute-start.6 = (f32[66,1,512]{2,1,0:T(1,128)S(1)}, f32[66,1,512]{2,1,0:T(1,128)S(1)}, u32[]{:S(2)}, u32[]{:S(2)}) collective-permute-start(f32[66,1,512]{2,1,0:T(1,128)S(1)} %get-tuple-element.37), channel_id=1, source_target_pairs={{1,0},{2,1},{3,2},{4,3},{5,4},{6,5},{7,6},{9,8},{10,9},{11,10},{12... | collective-permute-start | bytes 405512 | tf_op jit(solution)/shard_map/ppermute | solution.py:20
  91.3 7.1 %copy-start.7 = (f32[64,16,512]{2,1,0:T(8,128)S(1)}, f32[64,16,512]{2,1,0:T(8,128)}, u32[]{:S(2)}) copy-start(f32[64,16,512]{2,1,0:T(8,128)} %get-tuple-element.20) | copy-start | bytes 6291460
  91.3 7.1 %collective-permute-start.7 = (f32[66,1,512]{2,1,0:T(1,128)S(1)}, f32[66,1,512]{2,1,0:T(1,128)S(1)}, u32[]{:S(2)}, u32[]{:S(2)}) collective-permute-start(f32[66,1,512]{2,1,0:T(1,128)S(1)} %get-tuple-element.38), channel_id=1, source_target_pairs={{0,1},{1,2},{2,3},{3,4},{4,5},{5,6},{6,7},{8,9},{9,10},{10,11},{11... | collective-permute-start | bytes 405512 | tf_op jit(solution)/shard_map/ppermute | solution.py:17
  102.6 15.5 %copy-start = (f32[64,16,512]{2,1,0:T(8,128)}, f32[64,16,512]{2,1,0:T(8,128)S(1)}, u32[]{:S(2)}) copy-start(f32[64,16,512]{2,1,0:T(8,128)S(1)} %fusion.32) | copy-start | bytes 6291460
  102.7 5.0 %collective-permute-start.9 = (f32[1,16,512]{2,1,0:T(8,128)S(1)}, f32[1,16,512]{2,1,0:T(8,128)S(1)}, u32[]{:S(2)}, u32[]{:S(2)}) collective-permute-start(f32[1,16,512]{2,1,0:T(8,128)S(1)} %get-tuple-element.47), channel_id=1, source_target_pairs={{0,8},{8,16},{16,24},{1,9},{9,17},{17,25},{2,10},{10,18},{18,26},{... | collective-permute-start | bytes 98312 | tf_op jit(solution)/shard_map/ppermute | solution.py:17
  106.1 5.8 %collective-permute-start.8 = (f32[1,16,512]{2,1,0:T(8,128)S(1)}, f32[1,16,512]{2,1,0:T(8,128)S(1)}, u32[]{:S(2)}, u32[]{:S(2)}) collective-permute-start(f32[1,16,512]{2,1,0:T(8,128)S(1)} %get-tuple-element.48), channel_id=1, source_target_pairs={{8,0},{16,8},{24,16},{9,1},{17,9},{25,17},{10,2},{18,10},{26,18},{... | collective-permute-start | bytes 98312 | tf_op jit(solution)/shard_map/ppermute | solution.py:20
  112.1 5.9 %collective-permute-start.10 = (f32[66,1,512]{2,1,0:T(1,128)S(1)}, f32[66,1,512]{2,1,0:T(1,128)S(1)}, u32[]{:S(2)}, u32[]{:S(2)}) collective-permute-start(f32[66,1,512]{2,1,0:T(1,128)S(1)} %get-tuple-element.35), channel_id=1, source_target_pairs={{1,0},{2,1},{3,2},{4,3},{5,4},{6,5},{7,6},{9,8},{10,9},{11,10},{12... | collective-permute-start | bytes 405512 | tf_op jit(solution)/shard_map/ppermute | solution.py:20
  113.4 4.7 %collective-permute-start.11 = (f32[66,1,512]{2,1,0:T(1,128)S(1)}, f32[66,1,512]{2,1,0:T(1,128)S(1)}, u32[]{:S(2)}, u32[]{:S(2)}) collective-permute-start(f32[66,1,512]{2,1,0:T(1,128)S(1)} %get-tuple-element.36), channel_id=1, source_target_pairs={{0,1},{1,2},{2,3},{3,4},{4,5},{5,6},{6,7},{8,9},{9,10},{10,11},{11... | collective-permute-start | bytes 405512 | tf_op jit(solution)/shard_map/ppermute | solution.py:17
  158.4 35.0 %copy-start.5 = (f32[64,16,512]{2,1,0:T(8,128)}, f32[64,16,512]{2,1,0:T(8,128)S(1)}, u32[]{:S(2)}) copy-start(f32[64,16,512]{2,1,0:T(8,128)S(1)} %get-tuple-element.16) | copy-start | bytes 6291460
  158.4 4.6 %collective-permute-start.13 = (f32[1,16,512]{2,1,0:T(8,128)S(1)}, f32[1,16,512]{2,1,0:T(8,128)S(1)}, u32[]{:S(2)}, u32[]{:S(2)}) collective-permute-start(f32[1,16,512]{2,1,0:T(8,128)S(1)} %get-tuple-element.45), channel_id=1, source_target_pairs={{0,8},{8,16},{16,24},{1,9},{9,17},{17,25},{2,10},{10,18},{18,26},{... | collective-permute-start | bytes 98312 | tf_op jit(solution)/shard_map/ppermute | solution.py:17
  161.4 5.8 %collective-permute-start.12 = (f32[1,16,512]{2,1,0:T(8,128)S(1)}, f32[1,16,512]{2,1,0:T(8,128)S(1)}, u32[]{:S(2)}, u32[]{:S(2)}) collective-permute-start(f32[1,16,512]{2,1,0:T(8,128)S(1)} %get-tuple-element.46), channel_id=1, source_target_pairs={{8,0},{16,8},{24,16},{9,1},{17,9},{25,17},{10,2},{18,10},{26,18},{... | collective-permute-start | bytes 98312 | tf_op jit(solution)/shard_map/ppermute | solution.py:20
  167.5 5.3 %collective-permute-start.14 = (f32[66,1,512]{2,1,0:T(1,128)S(1)}, f32[66,1,512]{2,1,0:T(1,128)S(1)}, u32[]{:S(2)}, u32[]{:S(2)}) collective-permute-start(f32[66,1,512]{2,1,0:T(1,128)S(1)} %get-tuple-element.33), channel_id=1, source_target_pairs={{1,0},{2,1},{3,2},{4,3},{5,4},{6,5},{7,6},{9,8},{10,9},{11,10},{12... | collective-permute-start | bytes 405512 | tf_op jit(solution)/shard_map/ppermute | solution.py:20
  168.8 4.2 %copy-start.3 = (f32[64,16,512]{2,1,0:T(8,128)S(1)}, f32[64,16,512]{2,1,0:T(8,128)}, u32[]{:S(2)}) copy-start(f32[64,16,512]{2,1,0:T(8,128)} %copy-done.2) | copy-start | bytes 6291460
  168.8 4.1 %collective-permute-start.15 = (f32[66,1,512]{2,1,0:T(1,128)S(1)}, f32[66,1,512]{2,1,0:T(1,128)S(1)}, u32[]{:S(2)}, u32[]{:S(2)}) collective-permute-start(f32[66,1,512]{2,1,0:T(1,128)S(1)} %get-tuple-element.34), channel_id=1, source_target_pairs={{0,1},{1,2},{2,3},{3,4},{4,5},{5,6},{6,7},{8,9},{9,10},{10,11},{11... | collective-permute-start | bytes 405512 | tf_op jit(solution)/shard_map/ppermute | solution.py:17
  177.1 16.3 %copy-start.1 = (f32[64,16,512]{2,1,0:T(8,128)}, f32[64,16,512]{2,1,0:T(8,128)S(1)}, u32[]{:S(2)}) copy-start(f32[64,16,512]{2,1,0:T(8,128)S(1)} %fusion.15) | copy-start | bytes 6291460
  177.2 6.4 %collective-permute-start.17 = (f32[1,16,512]{2,1,0:T(8,128)S(1)}, f32[1,16,512]{2,1,0:T(8,128)S(1)}, u32[]{:S(2)}, u32[]{:S(2)}) collective-permute-start(f32[1,16,512]{2,1,0:T(8,128)S(1)} %get-tuple-element.39), channel_id=1, source_target_pairs={{0,8},{8,16},{16,24},{1,9},{9,17},{17,25},{2,10},{10,18},{18,26},{... | collective-permute-start | bytes 98312 | tf_op jit(solution)/shard_map/ppermute | solution.py:17
  181.8 5.9 %collective-permute-start.16 = (f32[1,16,512]{2,1,0:T(8,128)S(1)}, f32[1,16,512]{2,1,0:T(8,128)S(1)}, u32[]{:S(2)}, u32[]{:S(2)}) collective-permute-start(f32[1,16,512]{2,1,0:T(8,128)S(1)} %get-tuple-element.40), channel_id=1, source_target_pairs={{8,0},{16,8},{24,16},{9,1},{17,9},{25,17},{10,2},{18,10},{26,18},{... | collective-permute-start | bytes 98312 | tf_op jit(solution)/shard_map/ppermute | solution.py:20
  188.0 5.4 %collective-permute-start.18 = (f32[66,1,512]{2,1,0:T(1,128)S(1)}, f32[66,1,512]{2,1,0:T(1,128)S(1)}, u32[]{:S(2)}, u32[]{:S(2)}) collective-permute-start(f32[66,1,512]{2,1,0:T(1,128)S(1)} %get-tuple-element.31), channel_id=1, source_target_pairs={{1,0},{2,1},{3,2},{4,3},{5,4},{6,5},{7,6},{9,8},{10,9},{11,10},{12... | collective-permute-start | bytes 405512 | tf_op jit(solution)/shard_map/ppermute | solution.py:20
  189.3 4.1 %collective-permute-start.19 = (f32[66,1,512]{2,1,0:T(1,128)S(1)}, f32[66,1,512]{2,1,0:T(1,128)S(1)}, u32[]{:S(2)}, u32[]{:S(2)}) collective-permute-start(f32[66,1,512]{2,1,0:T(1,128)S(1)} %get-tuple-element.32), channel_id=1, source_target_pairs={{0,1},{1,2},{2,3},{3,4},{4,5},{5,6},{6,7},{8,9},{9,10},{10,11},{11... | collective-permute-start | bytes 405512 | tf_op jit(solution)/shard_map/ppermute | solution.py:17
  230.7 4.5 %copy-start.6 = (f32[64,16,512]{2,1,0:T(8,128)S(1)}, f32[64,16,512]{2,1,0:T(8,128)}, u32[]{:S(2)}) copy-start(f32[64,16,512]{2,1,0:T(8,128)} %copy-done.5) | copy-start | bytes 6291460
  230.7 4.4 %copy-start.8 = (f32[64,16,512]{2,1,0:T(8,128)S(1)}, f32[64,16,512]{2,1,0:T(8,128)}, u32[]{:S(2)}) copy-start(f32[64,16,512]{2,1,0:T(8,128)} %get-tuple-element.17) | copy-start | bytes 6291460
  230.7 4.4 %copy-start.9 = (f32[64,16,512]{2,1,0:T(8,128)S(1)}, f32[64,16,512]{2,1,0:T(8,128)}, u32[]{:S(2)}) copy-start(f32[64,16,512]{2,1,0:T(8,128)} %get-tuple-element.14) | copy-start | bytes 6291460
